TPU v7x, 128 devices: a whole 4x4x4 slice. The times are simulated.
128 devices in a mesh: tm: 2 (over core), space: 64 (over z, y, x).
Axes of the slice: x: 4, y: 4, z: 4, core: 2. Of those that a mesh axis runs over, the one named last changes fastest.
Arguments:
- fine: bfloat16 [8, 256, 256, 256], P('tm', 'space'), may hold values from -6 to 6
- coarse: bfloat16 [8, 128, 128, 256], P('tm', 'space'), may hold values from -6 to 6
- w_query: bfloat16 [256, 256], replicated, may hold values from -24 to 24
- w_key: bfloat16 [256, 256], replicated, may hold values from -0.375 to 0.375
- w_value: bfloat16 [256, 256], replicated, may hold values from -0.375 to 0.375
- w_out: bfloat16 [256, 256], replicated, may hold values from -0.375 to 0.375
- conv_first: bfloat16 [3, 3, 256, 256], replicated, may hold values from -0.125 to 0.125
- conv_second: bfloat16 [3, 3, 256, 256], replicated, may hold values from -0.125 to 0.125
Outputs:
- joined: bfloat16 [8, 256, 256, 256], P('tm', 'space')
All inputs are finite; a program needn't handle non-finite values.
Results may differ from a plain program's by a relative error of at most 0.009.
Values may be sent and summed in bfloat16 or wider, within the bound.
A program may use at most 128 MiB of HBM per device.

v0:
```python
import numpy as np
import jax
import jax.numpy as jnp
from jax import lax
from jax.experimental import pallas as pl
from jax.experimental.pallas import tpu as pltpu
from jax.sharding import PartitionSpec as P

HEADS = 8
C = 256
W = 256
FL = 4
RL = 4
BF = jnp.bfloat16
F32 = jnp.float32
MESH = pl.DeviceIdType.MESH


def tables():
    at = np.arange(256)
    col_of = (at % 16) * 16 + at // 16
    columns = np.zeros((256, 256), np.float32)
    columns[at, col_of] = 1.0
    channel = np.zeros((256, 256), np.float32)
    channel[at, (at % 32) * 8 + at // 32] = 1.0
    same = (at[:, None] // 128 == at[None, :] // 128) & (at[:, None] % 8 == at[None, :] % 8)
    heads = same.astype(np.float32)
    widen = np.zeros((256, 128), np.float32)
    for col in range(256):
        half = col // 2
        other = max(half - 1, 0) if col % 2 == 0 else min(half + 1, 127)
        widen[col, half] += 0.75
        widen[col, other] += 0.25
    widen = widen[col_of]
    none = np.zeros_like(widen)

    def pair(first, second):
        return np.concatenate([first * widen, second * widen], axis=1)

    stack = [columns, channel, channel.T, heads, pair(0.75, 0), pair(0.75, 0.25), pair(0.25, 0.75), pair(0, 0.75), pair(0.25, 0), pair(0, 0.25)]
    return np.stack(stack).astype(jnp.bfloat16)


def positions():
    half = C // 2
    inverse = np.exp(-np.log(10000.0) * 2.0 * np.arange(half) / C)
    angles = np.arange(8)[:, None] * inverse[None, :]
    return np.concatenate([np.sin(angles), np.cos(angles)], axis=1).astype(np.float32)[:, None, :]


def taps(ref, lead, first, rows):
    parts = []
    for dy in range(3):
        for dx in range(3):
            parts.append(ref[lead, first + dy : first + dy + rows, 16 * dx : 16 * dx + 256, :].reshape(rows * 256, C))
    return jnp.concatenate(parts, axis=1)


def pads(ref, lead, row):
    index = lax.broadcasted_iota(jnp.int32, (16, C), 0)
    last = ref[lead, row, 256:272, :].astype(F32)
    before = jnp.where(index == 0, 0.0, pltpu.roll(last, 1, axis=0))
    ref[lead, row, 0:16, :] = before.astype(BF)
    leading = ref[lead, row, 16:32, :].astype(F32)
    after = jnp.where(index == 15, 0.0, pltpu.roll(leading, 15, axis=0))
    ref[lead, row, 272:288, :] = after.astype(BF)


def kernel(
    spaces,
    fine_hbm, coarse_hbm, wq_hbm, wk_hbm, wv_hbm, wo_hbm, c1_hbm, c2_hbm, mats_hbm, pos_hbm,
    out_hbm,
    fin, cb, raw, mats, pos, cw1, cw2,
    wqp, wkv, wop, nbuf, fp, qs, kb, vb, att, xp, yp, acc, ob, psend, precv,
    load_sem, row_sem, nsend, nrecv, xsend, xrecv, tsend, trecv, out_sem,
):
    t = lax.axis_index("tm")
    s = lax.axis_index("space")
    has_up = s > 0
    has_down = s < spaces - 1

    def row_load(r):
        return pltpu.make_async_copy(fine_hbm.at[:, r], fin.at[:, r], row_sem.at[r])

    loads = [
        pltpu.make_async_copy(mats_hbm, mats, load_sem.at[0]),
        pltpu.make_async_copy(pos_hbm, pos, load_sem.at[1]),
        pltpu.make_async_copy(wq_hbm, raw.at[0], load_sem.at[2]),
        pltpu.make_async_copy(wk_hbm, raw.at[1], load_sem.at[3]),
        pltpu.make_async_copy(wv_hbm, raw.at[2], load_sem.at[4]),
        pltpu.make_async_copy(wo_hbm, raw.at[3], load_sem.at[5]),
        pltpu.make_async_copy(coarse_hbm, cb, load_sem.at[6]),
        pltpu.make_async_copy(c1_hbm, cw1, load_sem.at[7]),
        pltpu.make_async_copy(c2_hbm, cw2, load_sem.at[8]),
    ]
    loads[0].start()
    loads[1].start()
    row_load(0).start()
    row_load(3).start()
    for copy in loads[2:6]:
        copy.start()
    row_load(1).start()
    row_load(2).start()
    for copy in loads[6:]:
        copy.start()

    barrier = pltpu.get_barrier_semaphore()
    pl.semaphore_signal(barrier, inc=1, device_id=(1 - t, s), device_id_type=MESH)

    @pl.when(has_up)
    def _():
        pl.semaphore_signal(barrier, inc=1, device_id=(t, s - 1), device_id_type=MESH)

    @pl.when(has_down)
    def _():
        pl.semaphore_signal(barrier, inc=1, device_id=(t, s + 1), device_id_type=MESH)

    zero_row = jnp.zeros((FL, 288, C), BF)
    yp[:, 0] = zero_row
    yp[:, 5] = zero_row

    @pl.when(jnp.logical_not(has_up))
    def _():
        xp[:, 0] = zero_row

    @pl.when(jnp.logical_not(has_down))
    def _():
        xp[:, 5] = zero_row

    loads[0].wait()
    loads[1].wait()
    for copy in loads[2:6]:
        copy.wait()
    wqp[...] = jnp.dot(raw[0], mats[1], preferred_element_type=F32).astype(BF)
    wkv[:, 0:256] = jnp.dot(raw[1], mats[1], preferred_element_type=F32).astype(BF)
    wkv[:, 256:512] = jnp.dot(raw[2], mats[1], preferred_element_type=F32).astype(BF)
    wop[...] = jnp.dot(mats[2], raw[3], preferred_element_type=F32).astype(BF)

    pl.semaphore_wait(barrier, 1 + has_up.astype(jnp.int32) + has_down.astype(jnp.int32))

    def norm_copy(f, r):
        return pltpu.make_async_remote_copy(
            src_ref=nbuf.at[f, r], dst_ref=nbuf.at[f + FL, r],
            send_sem=nsend.at[f, r], recv_sem=nrecv.at[f, r],
            device_id=(1 - t, s), device_id_type=MESH)

    def normalize(rows):
        for r in rows:
            row_load(r).wait()

        def step(f, carry):
            for r in rows:
                moved = jnp.dot(mats[0], fin[f, r], preferred_element_type=F32)
                fp[f, r] = moved.astype(BF)
                hidden = moved + pos[t * FL + f]
                center = hidden - jnp.mean(hidden, axis=-1, keepdims=True)
                spread = jnp.mean(center * center, axis=-1, keepdims=True)
                nbuf[f, r] = (center * lax.rsqrt(spread + 1e-05)).astype(BF)
            for r in rows:
                norm_copy(f, r).start()
            return carry

        lax.fori_loop(0, FL, step, 0)

    def edge_copy(a, up):
        row, slot, to = (1, 5, s - 1) if up else (4, 0, s + 1)
        side = 0 if up else 1
        return pltpu.make_async_remote_copy(
            src_ref=xp.at[a, row, pl.ds(16, 256)], dst_ref=xp.at[a, slot, pl.ds(16, 256)],
            send_sem=xsend.at[side, a], recv_sem=xrecv.at[side, a],
            device_id=(t, to), device_id_type=MESH)

    def part_copy(a, up):
        side = 0 if up else 1
        to = s - 1 if up else s + 1
        return pltpu.make_async_remote_copy(
            src_ref=psend.at[side, a], dst_ref=precv.at[side, a],
            send_sem=tsend.at[side, a], recv_sem=trecv.at[side, a],
            device_id=(t, to), device_id_type=MESH)

    factor = float(np.log2(np.e) / np.sqrt(32.0))

    def keys(rows):
        def step(b, carry):
            for i, r in enumerate(rows):
                both = jnp.dot(nbuf[b, r], wkv[...], preferred_element_type=F32)
                kb[i, b] = both[:, 0:256].astype(BF)
                vb[i, b] = both[:, 256:512].astype(BF)
            return carry

        lax.fori_loop(0, FL, step, 0)
        for r in rows:
            for f in range(FL):
                norm_copy(f, r).wait_recv()
        lax.fori_loop(FL, 2 * FL, step, 0)

    def attend(rows, edges):
        def step(a, carry):
            for i, r in enumerate(rows):
                query = jnp.dot(nbuf[a, r], wqp[...], preferred_element_type=F32) * factor
                qs[i] = query.astype(BF)
                for blk in range(4):
                    px = slice(64 * blk, 64 * blk + 64)
                    q = qs[i, px]
                    lhs = []
                    for pair in range(4):
                        halves = []
                        for b in (2 * pair, 2 * pair + 1):
                            product = q * kb[i, b, px]
                            halves.append(product[:, 0:128] + product[:, 128:256])
                        lhs.append(jnp.concatenate(halves, axis=1))
                    both = jnp.dot(jnp.concatenate(lhs, axis=0), mats[3], preferred_element_type=F32)
                    scores = []
                    for b in range(8):
                        at = 64 * (b // 2)
                        scores.append(both[at : at + 64, 128 * (b % 2) : 128 * (b % 2) + 128])
                    largest = scores[0]
                    for entry in scores[1:]:
                        largest = jnp.maximum(largest, entry)
                    powers = [jnp.exp2(entry - largest) for entry in scores]
                    total = powers[0]
                    for entry in powers[1:]:
                        total = total + entry
                    inverse = 1.0 / total
                    low, high = [], []
                    for b in range(8):
                        weight = powers[b].astype(BF)
                        value = vb[i, b, px]
                        low.append(weight * value[:, 0:128])
                        high.append(weight * value[:, 128:256])
                    while len(low) > 1:
                        low = [low[j] + low[j + 1] for j in range(0, len(low), 2)]
                        high = [high[j] + high[j + 1] for j in range(0, len(high), 2)]
                    att[i, px, 0:128] = (low[0].astype(F32) * inverse).astype(BF)
                    att[i, px, 128:256] = (high[0].astype(F32) * inverse).astype(BF)
                branch = jnp.dot(att[i], wop[...], preferred_element_type=F32)
                moved = (fp[a, r].astype(F32) + branch).astype(BF)
                fp[a, r] = moved
                xp[a, r + 1, 16:272, :] = jnp.maximum(moved, jnp.zeros_like(moved))
            if edges:
                @pl.when(has_up)
                def _():
                    edge_copy(a, True).start()

                @pl.when(has_down)
                def _():
                    edge_copy(a, False).start()
            return carry

        lax.fori_loop(0, FL, step, 0)

    normalize((0, 3))
    normalize((1, 2))
    keys((0, 3))
    attend((0, 3), True)
    keys((1, 2))
    attend((1, 2), False)

    for copy in loads[6:]:
        copy.wait()

    def first_step(a, carry):
        for r in range(1, 5):
            pads(xp, a, r)

        @pl.when(has_up)
        def _():
            edge_copy(a, False).wait_recv()
            pads(xp, a, 0)

        @pl.when(has_down)
        def _():
            edge_copy(a, True).wait_recv()
            pads(xp, a, 5)

        weight = cw1[...].reshape(9 * C, C)
        for y in (0, 2):
            result = jnp.dot(taps(xp, a, y, 2), weight, preferred_element_type=F32)
            result = jnp.maximum(result, 0.0).astype(BF)
            yp[a, 1 + y : 3 + y, 16:272, :] = result.reshape(2, 256, C)
        for r in range(1, 5):
            pads(yp, a, r)
        near = cb[a].reshape(256, C)
        for side, row, dy in ((0, 1, 2), (1, 4, 0)):
            lhs = jnp.concatenate([yp[a, row, 16 * dx : 16 * dx + 256, :] for dx in range(3)], axis=1)
            part = jnp.dot(lhs, cw2[dy].reshape(3 * C, C), preferred_element_type=F32)
            part = part + jnp.dot(mats[8 + side], near, preferred_element_type=F32)
            psend[side, a] = part.astype(BF)

        @pl.when(has_up)
        def _():
            part_copy(a, True).start()

        @pl.when(has_down)
        def _():
            part_copy(a, False).start()

        return carry

    lax.fori_loop(0, FL, first_step, 0)

    def second_step(a, carry):
        weight = cw2[...].reshape(9 * C, C)
        near = cb[a].reshape(256, C)
        for y in (0, 2):
            result = jnp.dot(taps(yp, a, y, 2), weight, preferred_element_type=F32)
            for k in range(2):
                row = y + k
                up = jnp.dot(mats[4 + row], near, preferred_element_type=F32)
                value = result[256 * k : 256 * k + 256] + up + fp[a, row].astype(F32)
                if row in (1, 2):
                    ob[a, row] = value.astype(BF)
                else:
                    acc[a, row // 3] = value
        return carry

    lax.fori_loop(0, FL, second_step, 0)

    def edge_part(a, side):
        near = cb[a].reshape(256, C)
        precv[1 - side, a] = jnp.dot(mats[8 + side], near, preferred_element_type=F32).astype(BF)

    def last_step(a, carry):
        @pl.when(has_up)
        def _():
            part_copy(a, False).wait_recv()

        @pl.when(jnp.logical_not(has_up))
        def _():
            edge_part(a, 0)

        @pl.when(has_down)
        def _():
            part_copy(a, True).wait_recv()

        @pl.when(jnp.logical_not(has_down))
        def _():
            edge_part(a, 1)

        ob[a, 0] = (acc[a, 0] + precv[1, a].astype(F32)).astype(BF)
        ob[a, 3] = (acc[a, 1] + precv[0, a].astype(F32)).astype(BF)
        pltpu.make_async_copy(ob.at[a], out_hbm.at[a], out_sem.at[a]).start()
        return carry

    lax.fori_loop(0, FL, last_step, 0)

    def drain(a, carry):
        pltpu.make_async_copy(ob.at[a], out_hbm.at[a], out_sem.at[a]).wait()
        for r in range(RL):
            norm_copy(a, r).wait_send()

        @pl.when(has_up)
        def _():
            edge_copy(a, True).wait_send()
            part_copy(a, True).wait_send()

        @pl.when(has_down)
        def _():
            edge_copy(a, False).wait_send()
            part_copy(a, False).wait_send()

        return carry

    lax.fori_loop(0, FL, drain, 0)


def restore_kernel(mat, x, o):
    o[0, 0] = jnp.dot(mat[...], x[0, 0], preferred_element_type=F32).astype(BF)


def solution(mesh):
    spaces = mesh.shape["space"]
    constants = tables()
    place = positions()

    def local(fine, coarse, w_query, w_key, w_value, w_out, conv_first, conv_second):
        anywhere = pl.BlockSpec(memory_space=pl.ANY)
        dma = pltpu.SemaphoreType.DMA
        shape = (FL, RL, W, C)
        mats = jnp.asarray(constants)
        moved = pl.pallas_call(
            lambda *refs: kernel(spaces, *refs),
            out_shape=jax.ShapeDtypeStruct(shape, BF),
            in_specs=[anywhere] * 10,
            out_specs=anywhere,
            scratch_shapes=[
                pltpu.VMEM(shape, BF),
                pltpu.VMEM((FL, 2, 128, C), BF),
                pltpu.VMEM((4, C, C), BF),
                pltpu.VMEM((10, 256, 256), BF),
                pltpu.VMEM((8, 1, C), F32),
                pltpu.VMEM((3, 3, C, C), BF),
                pltpu.VMEM((3, 3, C, C), BF),
                pltpu.VMEM((C, C), BF),
                pltpu.VMEM((C, 2 * C), BF),
                pltpu.VMEM((C, C), BF),
                pltpu.VMEM((2 * FL, RL, W, C), BF),
                pltpu.VMEM(shape, BF),
                pltpu.VMEM((2, W, C), BF),
                pltpu.VMEM((2, 2 * FL, W, C), BF),
                pltpu.VMEM((2, 2 * FL, W, C), BF),
                pltpu.VMEM((2, W, C), BF),
                pltpu.VMEM((FL, RL + 2, W + 32, C), BF),
                pltpu.VMEM((FL, RL + 2, W + 32, C), BF),
                pltpu.VMEM((FL, 2, W, C), F32),
                pltpu.VMEM(shape, BF),
                pltpu.VMEM((2, FL, W, C), BF),
                pltpu.VMEM((2, FL, W, C), BF),
                dma((9,)),
                dma((RL,)),
                dma((FL, RL)),
                dma((FL, RL)),
                dma((2, FL)),
                dma((2, FL)),
                dma((2, FL)),
                dma((2, FL)),
                dma((FL,)),
            ],
            compiler_params=pltpu.CompilerParams(
                collective_id=0, has_side_effects=True, vmem_limit_bytes=60 * 1024 * 1024),
            name="fused",
        )(fine, coarse, w_query, w_key, w_value, w_out, conv_first, conv_second, mats, jnp.asarray(place))
        block = pl.BlockSpec((1, 1, W, C), lambda i, j: (i, j, 0, 0))
        return pl.pallas_call(
            restore_kernel,
            grid=(FL, RL),
            out_shape=jax.ShapeDtypeStruct(shape, BF),
            in_specs=[pl.BlockSpec((None, 256, 256), lambda i, j: (0, 0, 0)), block],
            out_specs=block,
            name="restore",
        )(mats, moved)

    return jax.shard_map(
        local,
        mesh=mesh,
        in_specs=(P("tm", "space", None, None), P("tm", "space", None, None), P(), P(), P(), P(), P(), P()),
        out_specs=P("tm", "space", None, None),
        check_vma=False,
    )
```

profile of v0, /device:TPU:96, one launch (start us, length us, event | category | flops | bytes accessed | tf_op | source)
XLA Modules:
  0.0 51.0 jit_solution(7193994769993497961)
XLA Ops:
  0.0 40.3 %fused.1.x = bf16[4,4,256,256]{3,2,1,0:T(8,128)(2,1)} custom-call(bf16[4,4,256,256]{3,2,1,0:T(8,128)(2,1)} %refs_0_.1, bf16[4,2,128,256]{3,2,1,0:T(8,128)(2,1)} %refs_1_.1, bf16[256,256]{1,0:T(8,128)(2,1)} %refs_2_.1, bf16[256,256]{1,0:T(8,128)(2,1)} %refs_3_.1, bf16[256,256]{1,0:T(8,128)(2,1)} %refs_4_.1, bf16[256,256]{1,0:T(8,128)(2,1)} %refs_5_.1, ...), custom_call_target="tpu_custom_call" | custom-call | tf_op jit(solution)/shard_map/fused/pallas_call | solution.py:381
  40.3 10.6 %restore.1 = bf16[4,4,256,256]{3,2,1,0:T(8,128)(2,1)} custom-call(bf16[10,256,256]{2,1,0:T(8,128)(2,1)} %constant.4.clone.refs_8_.mat, bf16[4,4,256,256]{3,2,1,0:T(8,128)(2,1)} %fused.1.x), custom_call_target="tpu_custom_call" | custom-call | tf_op jit(solution)/shard_map/restore/pallas_call | solution.py:424
where the time goes:
time: 51.3 us; the launch traced here: 51 us
  Pallas kernels  51 us (99%)
    pallas_call x1, Pallas kernels, local(): pl.pallas_call(lambda *refs: kernel(spaces, *refs), out_shape=jax.ShapeDt...  40.3 us
    pallas_call x1, Pallas kernels, local(): pl.pallas_call(restore_kernel, grid=(FL, RL), out_shape=jax.ShapeDtypeStr...  10.6 us

commit v1 on v0

--- a/solution.py
+++ b/solution.py
@@ -69,10 +69,10 @@
 def kernel(
     spaces,
     fine_hbm, coarse_hbm, wq_hbm, wk_hbm, wv_hbm, wo_hbm, c1_hbm, c2_hbm, mats_hbm, pos_hbm,
-    out_hbm,
+    ob,
     fin, cb, raw, mats, pos, cw1, cw2,
-    wqp, wkv, wop, nbuf, fp, qs, kb, vb, att, xp, yp, acc, ob, psend, precv,
-    load_sem, row_sem, nsend, nrecv, xsend, xrecv, tsend, trecv, out_sem,
+    wqp, wkv, wop, nbuf, fp, qs, kb, vb, att, xp, yp, acc, psend, precv,
+    load_sem, row_sem, nsend, nrecv, xsend, xrecv, tsend, trecv,
 ):
     t = lax.axis_index("tm")
     s = lax.axis_index("space")
@@ -127,16 +127,18 @@
     def _():
         xp[:, 5] = zero_row
 
-    loads[0].wait()
-    loads[1].wait()
-    for copy in loads[2:6]:
-        copy.wait()
+    with jax.named_scope("load_wait"):
+        loads[0].wait()
+        loads[1].wait()
+        for copy in loads[2:6]:
+            copy.wait()
     wqp[...] = jnp.dot(raw[0], mats[1], preferred_element_type=F32).astype(BF)
     wkv[:, 0:256] = jnp.dot(raw[1], mats[1], preferred_element_type=F32).astype(BF)
     wkv[:, 256:512] = jnp.dot(raw[2], mats[1], preferred_element_type=F32).astype(BF)
     wop[...] = jnp.dot(mats[2], raw[3], preferred_element_type=F32).astype(BF)
 
-    pl.semaphore_wait(barrier, 1 + has_up.astype(jnp.int32) + has_down.astype(jnp.int32))
+    with jax.named_scope("barrier"):
+        pl.semaphore_wait(barrier, 1 + has_up.astype(jnp.int32) + has_down.astype(jnp.int32))
 
     def norm_copy(f, r):
         return pltpu.make_async_remote_copy(
@@ -148,19 +150,20 @@
         for r in rows:
             row_load(r).wait()
 
-        def step(f, carry):
-            for r in rows:
-                moved = jnp.dot(mats[0], fin[f, r], preferred_element_type=F32)
+        def step(pair, carry):
+            units = [(2 * pair + k, r) for k in range(2) for r in rows]
+            placed = [jnp.dot(mats[0], fin[f, r], preferred_element_type=F32) for f, r in units]
+            for (f, r), moved in zip(units, placed):
                 fp[f, r] = moved.astype(BF)
                 hidden = moved + pos[t * FL + f]
                 center = hidden - jnp.mean(hidden, axis=-1, keepdims=True)
                 spread = jnp.mean(center * center, axis=-1, keepdims=True)
                 nbuf[f, r] = (center * lax.rsqrt(spread + 1e-05)).astype(BF)
-            for r in rows:
+            for f, r in units:
                 norm_copy(f, r).start()
             return carry
 
-        lax.fori_loop(0, FL, step, 0)
+        lax.fori_loop(0, FL // 2, step, 0)
 
     def edge_copy(a, up):
         row, slot, to = (1, 5, s - 1) if up else (4, 0, s + 1)
@@ -181,27 +184,36 @@
     factor = float(np.log2(np.e) / np.sqrt(32.0))
 
     def keys(rows):
-        def step(b, carry):
-            for i, r in enumerate(rows):
-                both = jnp.dot(nbuf[b, r], wkv[...], preferred_element_type=F32)
-                kb[i, b] = both[:, 0:256].astype(BF)
-                vb[i, b] = both[:, 256:512].astype(BF)
+        def step(own, pair, carry):
+            frames = [2 * pair + k for k in range(2)]
+            results, queries = [], []
+            for b in frames:
+                stacked = jnp.concatenate([nbuf[b, r] for r in rows], axis=0)
+                results.append(jnp.dot(stacked, wkv[...], preferred_element_type=F32))
+                if own:
+                    queries.append(jnp.dot(stacked, wqp[...], preferred_element_type=F32))
+            for b, both in zip(frames, results):
+                for i in range(2):
+                    kb[i, b] = both[256 * i : 256 * i + 256, 0:256].astype(BF)
+                    vb[i, b] = both[256 * i : 256 * i + 256, 256:512].astype(BF)
+            for b, query in zip(frames, queries):
+                for i in range(2):
+                    qs[i, b] = (query[256 * i : 256 * i + 256] * factor).astype(BF)
             return carry
 
-        lax.fori_loop(0, FL, step, 0)
-        for r in rows:
-            for f in range(FL):
-                norm_copy(f, r).wait_recv()
-        lax.fori_loop(FL, 2 * FL, step, 0)
+        lax.fori_loop(0, FL // 2, lambda i, c: step(True, i, c), 0)
+        with jax.named_scope("norm_wait"):
+            for r in rows:
+                for f in range(FL):
+                    norm_copy(f, r).wait_recv()
+        lax.fori_loop(FL // 2, FL, lambda i, c: step(False, i, c), 0)
 
     def attend(rows, edges):
         def step(a, carry):
             for i, r in enumerate(rows):
-                query = jnp.dot(nbuf[a, r], wqp[...], preferred_element_type=F32) * factor
-                qs[i] = query.astype(BF)
                 for blk in range(4):
                     px = slice(64 * blk, 64 * blk + 64)
-                    q = qs[i, px]
+                    q = qs[i, a, px]
                     lhs = []
                     for pair in range(4):
                         halves = []
@@ -249,12 +261,18 @@
 
         lax.fori_loop(0, FL, step, 0)
 
-    normalize((0, 3))
-    normalize((1, 2))
-    keys((0, 3))
-    attend((0, 3), True)
-    keys((1, 2))
-    attend((1, 2), False)
+    with jax.named_scope("norm03"):
+        normalize((0, 3))
+    with jax.named_scope("norm12"):
+        normalize((1, 2))
+    with jax.named_scope("keys03"):
+        keys((0, 3))
+    with jax.named_scope("attend03"):
+        attend((0, 3), True)
+    with jax.named_scope("keys12"):
+        keys((1, 2))
+    with jax.named_scope("attend12"):
+        attend((1, 2), False)
 
     for copy in loads[6:]:
         copy.wait()
@@ -265,12 +283,14 @@
 
         @pl.when(has_up)
         def _():
-            edge_copy(a, False).wait_recv()
+            with jax.named_scope("edge_wait_up"):
+                edge_copy(a, False).wait_recv()
             pads(xp, a, 0)
 
         @pl.when(has_down)
         def _():
-            edge_copy(a, True).wait_recv()
+            with jax.named_scope("edge_wait_down"):
+                edge_copy(a, True).wait_recv()
             pads(xp, a, 5)
 
         weight = cw1[...].reshape(9 * C, C)
@@ -297,24 +317,28 @@
 
         return carry
 
-    lax.fori_loop(0, FL, first_step, 0)
+    with jax.named_scope("first"):
+        lax.fori_loop(0, FL, first_step, 0)
 
     def second_step(a, carry):
-        weight = cw2[...].reshape(9 * C, C)
         near = cb[a].reshape(256, C)
-        for y in (0, 2):
-            result = jnp.dot(taps(yp, a, y, 2), weight, preferred_element_type=F32)
-            for k in range(2):
-                row = y + k
-                up = jnp.dot(mats[4 + row], near, preferred_element_type=F32)
-                value = result[256 * k : 256 * k + 256] + up + fp[a, row].astype(F32)
-                if row in (1, 2):
-                    ob[a, row] = value.astype(BF)
-                else:
-                    acc[a, row // 3] = value
+        inner = jnp.dot(taps(yp, a, 1, 2), cw2[...].reshape(9 * C, C), preferred_element_type=F32)
+        outer = []
+        for row, first, dys in ((0, 1, (1, 2)), (3, 3, (0, 1))):
+            parts = [yp[a, first + k, 16 * dx : 16 * dx + 256, :] for k in range(2) for dx in range(3)]
+            weight = cw2[dys[0] : dys[0] + 2].reshape(6 * C, C)
+            outer.append(jnp.dot(jnp.concatenate(parts, axis=1), weight, preferred_element_type=F32))
+        up = jnp.dot(mats[4:8].reshape(4 * 256, 256), near, preferred_element_type=F32)
+        for row, value in ((1, inner[0:256]), (2, inner[256:512]), (0, outer[0]), (3, outer[1])):
+            value = value + up[256 * row : 256 * row + 256] + fp[a, row].astype(F32)
+            if row in (1, 2):
+                fp[a, row] = value.astype(BF)
+            else:
+                acc[a, row // 3] = value
         return carry
 
-    lax.fori_loop(0, FL, second_step, 0)
+    with jax.named_scope("second"):
+        lax.fori_loop(0, FL, second_step, 0)
 
     def edge_part(a, side):
         near = cb[a].reshape(256, C)
@@ -323,7 +347,8 @@
     def last_step(a, carry):
         @pl.when(has_up)
         def _():
-            part_copy(a, False).wait_recv()
+            with jax.named_scope("part_wait_up"):
+                part_copy(a, False).wait_recv()
 
         @pl.when(jnp.logical_not(has_up))
         def _():
@@ -331,21 +356,29 @@
 
         @pl.when(has_down)
         def _():
-            part_copy(a, True).wait_recv()
+            with jax.named_scope("part_wait_down"):
+                part_copy(a, True).wait_recv()
 
         @pl.when(jnp.logical_not(has_down))
         def _():
             edge_part(a, 1)
 
-        ob[a, 0] = (acc[a, 0] + precv[1, a].astype(F32)).astype(BF)
-        ob[a, 3] = (acc[a, 1] + precv[0, a].astype(F32)).astype(BF)
-        pltpu.make_async_copy(ob.at[a], out_hbm.at[a], out_sem.at[a]).start()
+        for row, side in ((0, 1), (3, 0)):
+            value = (acc[a, row // 3] + precv[side, a].astype(F32)).astype(BF)
+            ob[a, row] = jnp.dot(mats[0], value, preferred_element_type=F32).astype(BF)
         return carry
 
-    lax.fori_loop(0, FL, last_step, 0)
+    def restore_step(a, carry):
+        for row in (1, 2):
+            ob[a, row] = jnp.dot(mats[0], fp[a, row], preferred_element_type=F32).astype(BF)
+        return carry
+
+    with jax.named_scope("restore"):
+        lax.fori_loop(0, FL, restore_step, 0)
+    with jax.named_scope("last"):
+        lax.fori_loop(0, FL, last_step, 0)
 
     def drain(a, carry):
-        pltpu.make_async_copy(ob.at[a], out_hbm.at[a], out_sem.at[a]).wait()
         for r in range(RL):
             norm_copy(a, r).wait_send()
 
@@ -361,11 +394,8 @@
 
         return carry
 
-    lax.fori_loop(0, FL, drain, 0)
-
-
-def restore_kernel(mat, x, o):
-    o[0, 0] = jnp.dot(mat[...], x[0, 0], preferred_element_type=F32).astype(BF)
+    with jax.named_scope("drain"):
+        lax.fori_loop(0, FL, drain, 0)
 
 
 def solution(mesh):
@@ -380,9 +410,9 @@
         mats = jnp.asarray(constants)
         moved = pl.pallas_call(
             lambda *refs: kernel(spaces, *refs),
-            out_shape=jax.ShapeDtypeStruct(shape, BF),
+            out_shape=pltpu.VMEM(shape, BF),
             in_specs=[anywhere] * 10,
-            out_specs=anywhere,
+            out_specs=pl.BlockSpec(memory_space=pltpu.VMEM),
             scratch_shapes=[
                 pltpu.VMEM(shape, BF),
                 pltpu.VMEM((FL, 2, 128, C), BF),
@@ -396,14 +426,13 @@
                 pltpu.VMEM((C, C), BF),
                 pltpu.VMEM((2 * FL, RL, W, C), BF),
                 pltpu.VMEM(shape, BF),
-                pltpu.VMEM((2, W, C), BF),
+                pltpu.VMEM((2, FL, W, C), BF),
                 pltpu.VMEM((2, 2 * FL, W, C), BF),
                 pltpu.VMEM((2, 2 * FL, W, C), BF),
                 pltpu.VMEM((2, W, C), BF),
                 pltpu.VMEM((FL, RL + 2, W + 32, C), BF),
                 pltpu.VMEM((FL, RL + 2, W + 32, C), BF),
                 pltpu.VMEM((FL, 2, W, C), F32),
-                pltpu.VMEM(shape, BF),
                 pltpu.VMEM((2, FL, W, C), BF),
                 pltpu.VMEM((2, FL, W, C), BF),
                 dma((9,)),
@@ -414,21 +443,24 @@
                 dma((2, FL)),
                 dma((2, FL)),
                 dma((2, FL)),
-                dma((FL,)),
             ],
             compiler_params=pltpu.CompilerParams(
                 collective_id=0, has_side_effects=True, vmem_limit_bytes=60 * 1024 * 1024),
             name="fused",
         )(fine, coarse, w_query, w_key, w_value, w_out, conv_first, conv_second, mats, jnp.asarray(place))
-        block = pl.BlockSpec((1, 1, W, C), lambda i, j: (i, j, 0, 0))
+        def emit(x, o, sem):
+            copy = pltpu.make_async_copy(x, o, sem)
+            copy.start()
+            copy.wait()
+
         return pl.pallas_call(
-            restore_kernel,
-            grid=(FL, RL),
+            emit,
             out_shape=jax.ShapeDtypeStruct(shape, BF),
-            in_specs=[pl.BlockSpec((None, 256, 256), lambda i, j: (0, 0, 0)), block],
-            out_specs=block,
-            name="restore",
-        )(mats, moved)
+            in_specs=[pl.BlockSpec(memory_space=pltpu.VMEM)],
+            out_specs=anywhere,
+            scratch_shapes=[dma],
+            name="emit",
+        )(pltpu.with_memory_space_constraint(moved, pltpu.VMEM))
 
     return jax.shard_map(
         local,

time: 51.3 us -> 38.3 us (0.75)
  Pallas kernels: 51 us -> 38.2 us
    pallas_call x2, Pallas kernels: 51 us -> 38.2 us  [the longest x1 36.9 us: local(): pl.pallas_call(lambda *refs: kernel(spaces, *refs), out_shape=pltpu.VMEM(...]
where the time goes in v1:
time: 38.3 us; the launch traced here: 38.2 us
  Pallas kernels  38.2 us (100%)
    pallas_call x1, Pallas kernels, local(): pl.pallas_call(lambda *refs: kernel(spaces, *refs), out_shape=pltpu.VMEM(...  36.9 us
    pallas_call x1, Pallas kernels, local(): pl.pallas_call(emit, out_shape=jax.ShapeDtypeStruct(shape, BF), in_specs=...  1.33 us

profile of v1, /device:TPU:96, one launch (start us, length us, event | category | flops | bytes accessed | tf_op | source)
XLA Modules:
  0.0 38.2 jit_solution(12675631346953772656)
XLA Ops:
  0.0 36.9 %fused.1.x = bf16[4,4,256,256]{3,2,1,0:T(8,128)(2,1)S(1)} custom-call(bf16[4,4,256,256]{3,2,1,0:T(8,128)(2,1)} %refs_0_.1, bf16[4,2,128,256]{3,2,1,0:T(8,128)(2,1)} %refs_1_.1, bf16[256,256]{1,0:T(8,128)(2,1)} %refs_2_.1, bf16[256,256]{1,0:T(8,128)(2,1)} %refs_3_.1, bf16[256,256]{1,0:T(8,128)(2,1)} %refs_4_.1, bf16[256,256]{1,0:T(8,128)(2,1)} %refs_5_.1, ...), custom_call_target="tpu_custom_call" | custom-call | tf_op jit(solution)/shard_map/fused/pallas_call | solution.py:411
  36.9 1.3 %emit.1 = bf16[4,4,256,256]{3,2,1,0:T(8,128)(2,1)} custom-call(bf16[4,4,256,256]{3,2,1,0:T(8,128)(2,1)S(1)} %fused.1.x), custom_call_target="tpu_custom_call" | custom-call | tf_op jit(solution)/shard_map/emit/pallas_call | solution.py:456

commit v2 on v1

v2 whole, which is shorter than its diff:
```python
import numpy as np
import jax
import jax.numpy as jnp
from jax import lax
from jax.experimental import pallas as pl
from jax.experimental.pallas import tpu as pltpu
from jax.sharding import PartitionSpec as P

HEADS = 8
C = 256
W = 256
FL = 4
RL = 4
BF = jnp.bfloat16
F32 = jnp.float32
MESH = pl.DeviceIdType.MESH


def tables():
    at = np.arange(256)
    col_of = (at % 16) * 16 + at // 16
    columns = np.zeros((256, 256), np.float32)
    columns[at, col_of] = 1.0
    channel = np.zeros((256, 256), np.float32)
    channel[at, (at % 32) * 8 + at // 32] = 1.0
    same = (at[:, None] // 128 == at[None, :] // 128) & (at[:, None] % 8 == at[None, :] % 8)
    heads = same.astype(np.float32)
    widen = np.zeros((256, 128), np.float32)
    for col in range(256):
        half = col // 2
        other = max(half - 1, 0) if col % 2 == 0 else min(half + 1, 127)
        widen[col, half] += 0.75
        widen[col, other] += 0.25
    widen = widen[col_of]
    none = np.zeros_like(widen)

    def pair(first, second):
        return np.concatenate([first * widen, second * widen], axis=1)

    stack = [columns, channel, channel.T, heads, pair(0.75, 0), pair(0.75, 0.25), pair(0.25, 0.75), pair(0, 0.75), pair(0.25, 0), pair(0, 0.25)]
    return np.stack(stack).astype(jnp.bfloat16)


def positions():
    half = C // 2
    inverse = np.exp(-np.log(10000.0) * 2.0 * np.arange(half) / C)
    angles = np.arange(8)[:, None] * inverse[None, :]
    return np.concatenate([np.sin(angles), np.cos(angles)], axis=1).astype(np.float32)[:, None, :]


def taps(ref, lead, first, rows):
    parts = []
    for dy in range(3):
        for dx in range(3):
            parts.append(ref[lead, first + dy : first + dy + rows, 16 * dx : 16 * dx + 256, :].reshape(rows * 256, C))
    return jnp.concatenate(parts, axis=1)


def pads(ref, lead, row):
    index = lax.broadcasted_iota(jnp.int32, (16, C), 0)
    last = ref[lead, row, 256:272, :].astype(F32)
    before = jnp.where(index == 0, 0.0, pltpu.roll(last, 1, axis=0))
    ref[lead, row, 0:16, :] = before.astype(BF)
    leading = ref[lead, row, 16:32, :].astype(F32)
    after = jnp.where(index == 15, 0.0, pltpu.roll(leading, 15, axis=0))
    ref[lead, row, 272:288, :] = after.astype(BF)


def kernel(
    spaces,
    fine_hbm, coarse_hbm, wq_hbm, wk_hbm, wv_hbm, wo_hbm, c1_hbm, c2_hbm, mats_hbm, pos_hbm,
    ob,
    fin, cb, raw, mats, pos, cw1, cw2,
    wqp, wkv, wop, nbuf, fp, qs, kb, vb, att, xp, yp, acc, psend, precv,
    load_sem, row_sem, nsend, nrecv, xsend, xrecv, tsend, trecv, near_sem, far_sem,
):
    t = lax.axis_index("tm")
    s = lax.axis_index("space")
    has_up = s > 0
    has_down = s < spaces - 1

    def row_load(r):
        return pltpu.make_async_copy(fine_hbm.at[:, r], fin.at[:, r], row_sem.at[r])

    loads = [
        pltpu.make_async_copy(mats_hbm.at[0], mats.at[0], load_sem.at[0]),
        pltpu.make_async_copy(pos_hbm, pos, load_sem.at[1]),
        pltpu.make_async_copy(wq_hbm, raw.at[0], load_sem.at[2]),
        pltpu.make_async_copy(wk_hbm, raw.at[1], load_sem.at[3]),
        pltpu.make_async_copy(wv_hbm, raw.at[2], load_sem.at[4]),
        pltpu.make_async_copy(wo_hbm, raw.at[3], load_sem.at[5]),
        pltpu.make_async_copy(mats_hbm.at[pl.ds(1, 9)], mats.at[pl.ds(1, 9)], load_sem.at[9]),
        pltpu.make_async_copy(coarse_hbm, cb, load_sem.at[6]),
        pltpu.make_async_copy(c1_hbm, cw1, load_sem.at[7]),
        pltpu.make_async_copy(c2_hbm, cw2, load_sem.at[8]),
    ]
    loads[0].start()
    loads[1].start()
    row_load(0).start()
    row_load(3).start()

    barrier = pltpu.get_barrier_semaphore()

    @pl.when(t == 1)
    def _():
        pl.semaphore_signal(barrier, inc=1, device_id=(1 - t, s), device_id_type=MESH)

    for copy in loads[2:7]:
        copy.start()
    row_load(1).start()
    row_load(2).start()
    for copy in loads[7:]:
        copy.start()

    @pl.when(t == 0)
    def _():
        pl.semaphore_wait(barrier, 1)
        pl.semaphore_signal(near_sem, inc=1, device_id=(1 - t, s), device_id_type=MESH)

    @pl.when(t == 1)
    def _():
        pl.semaphore_wait(near_sem, 1)

    @pl.when(jnp.logical_and(t == 1, has_up))
    def _():
        pl.semaphore_signal(barrier, inc=1, device_id=(t, s - 1), device_id_type=MESH)

    @pl.when(jnp.logical_and(t == 1, has_down))
    def _():
        pl.semaphore_signal(barrier, inc=1, device_id=(t, s + 1), device_id_type=MESH)

    def meet_neighbours():
        @pl.when(t == 1)
        def _():
            pl.semaphore_wait(barrier, has_up.astype(jnp.int32) + has_down.astype(jnp.int32))
            pl.semaphore_signal(far_sem, inc=1, device_id=(1 - t, s), device_id_type=MESH)

        @pl.when(t == 0)
        def _():
            pl.semaphore_wait(far_sem, 1)

    zero_row = jnp.zeros((FL, 288, C), BF)

    @pl.when(jnp.logical_not(has_up))
    def _():
        xp[:, 0] = zero_row

    @pl.when(jnp.logical_not(has_down))
    def _():
        xp[:, 5] = zero_row

    def norm_copy(k):
        r = (0, 3, 0, 3, 1, 2)[k]
        px = pl.ds((0, 0, 128, 128, 0, 0)[k], 128 if k < 4 else 256)
        return pltpu.make_async_remote_copy(
            src_ref=nbuf.at[pl.ds(0, FL), r, px], dst_ref=nbuf.at[pl.ds(FL, FL), r, px],
            send_sem=nsend.at[k], recv_sem=nrecv.at[k],
            device_id=(1 - t, s), device_id_type=MESH)

    def normalize(units, start, count):
        px = slice(start, start + count)
        placed = [jnp.dot(mats[0, px], fin[f, r], preferred_element_type=F32) for f, r in units]
        for (f, r), moved in zip(units, placed):
            fp[f, r, px] = moved.astype(BF)
            hidden = moved + pos[t * FL + f]
            center = hidden - jnp.mean(hidden, axis=-1, keepdims=True)
            spread = jnp.mean(center * center, axis=-1, keepdims=True)
            nbuf[f, r, px] = (center * lax.rsqrt(spread + 1e-05)).astype(BF)

    def edge_copy(a, up, h):
        row, slot, to = (1, 5, s - 1) if up else (4, 0, s + 1)
        side = 0 if up else 1
        px = pl.ds(16 + 128 * h, 128)
        return pltpu.make_async_remote_copy(
            src_ref=xp.at[a, row, px], dst_ref=xp.at[a, slot, px],
            send_sem=xsend.at[side, a, h], recv_sem=xrecv.at[side, a, h],
            device_id=(t, to), device_id_type=MESH)

    def part_copy(a, up):
        side = 0 if up else 1
        to = s - 1 if up else s + 1
        return pltpu.make_async_remote_copy(
            src_ref=psend.at[side, a], dst_ref=precv.at[side, a],
            send_sem=tsend.at[side, a], recv_sem=trecv.at[side, a],
            device_id=(t, to), device_id_type=MESH)

    factor = float(np.log2(np.e) / np.sqrt(32.0))

    def project(rows, frames, own, start, count):
        px = slice(start, start + count)
        units = [(b, r) for b in frames for r in rows]
        stacked = jnp.concatenate([nbuf[b, r, px] for b, r in units], axis=0)
        both = jnp.dot(stacked, wkv[...], preferred_element_type=F32)
        if own:
            query = jnp.dot(stacked, wqp[...], preferred_element_type=F32)
        for i, (b, r) in enumerate(units):
            at = slice(count * i, count * i + count)
            kb[r, b, px] = both[at, 0:256].astype(BF)
            vb[r, b, px] = both[at, 256:512].astype(BF)
            if own:
                qs[r, b, px] = (query[at] * factor).astype(BF)

    def weigh(a, r, start, into):
        px = slice(start, start + 64)
        out = slice(into, into + 64)
        q = qs[r, a, px]
        lhs = []
        for pair in range(4):
            halves = []
            for b in (2 * pair, 2 * pair + 1):
                product = q * kb[r, b, px]
                halves.append(product[:, 0:128] + product[:, 128:256])
            lhs.append(jnp.concatenate(halves, axis=1))
        both = jnp.dot(jnp.concatenate(lhs, axis=0), mats[3], preferred_element_type=F32)
        scores = []
        for b in range(8):
            at = 64 * (b // 2)
            scores.append(both[at : at + 64, 128 * (b % 2) : 128 * (b % 2) + 128])
        largest = scores[0]
        for entry in scores[1:]:
            largest = jnp.maximum(largest, entry)
        powers = [jnp.exp2(entry - largest) for entry in scores]
        total = powers[0]
        for entry in powers[1:]:
            total = total + entry
        inverse = 1.0 / total
        low, high = [], []
        for b in range(8):
            weight = powers[b].astype(BF)
            value = vb[r, b, px]
            low.append(weight * value[:, 0:128])
            high.append(weight * value[:, 128:256])
        while len(low) > 1:
            low = [low[j] + low[j + 1] for j in range(0, len(low), 2)]
            high = [high[j] + high[j + 1] for j in range(0, len(high), 2)]
        att[out, 0:128] = (low[0].astype(F32) * inverse).astype(BF)
        att[out, 128:256] = (high[0].astype(F32) * inverse).astype(BF)

    def attend(units, count, beside=()):
        beside = list(beside)
        into = 0
        for a, r, start in units:
            for px in range(start, start + count, 64):
                weigh(a, r, px, into)
                into += 64
                if into % 128 == 0 and beside:
                    beside.pop(0)()
        for run in beside:
            run()
        branch = jnp.dot(att[...], wop[...], preferred_element_type=F32)
        for i, (a, r, start) in enumerate(units):
            px = slice(start, start + count)
            moved = (fp[a, r, px].astype(F32) + branch[count * i : count * i + count]).astype(BF)
            fp[a, r, px] = moved
            xp[a, r + 1, 16 + start : 16 + start + count, :] = jnp.maximum(moved, jnp.zeros_like(moved))

    def send_edges(a, h):
        @pl.when(has_up)
        def _():
            edge_copy(a, True, h).start()

        @pl.when(has_down)
        def _():
            edge_copy(a, False, h).start()

    def wait_norms(ks):
        with jax.named_scope("norm_wait"):
            for k in ks:
                norm_copy(k).wait_recv()

    def first_wait(a):
        @pl.when(has_up)
        def _():
            with jax.named_scope("edge_wait_up"):
                for h in range(2):
                    edge_copy(a, False, h).wait_recv()

        @pl.when(has_down)
        def _():
            with jax.named_scope("edge_wait_down"):
                for h in range(2):
                    edge_copy(a, True, h).wait_recv()

    def first_rows(a):
        weight = cw1[...].reshape(9 * C, C)

        def run(y):
            result = jnp.dot(taps(xp, a, y, 1), weight, preferred_element_type=F32)
            yp[a, 1 + y, 16:272, :] = jnp.maximum(result, 0.0).astype(BF)

        return [lambda y=y: run(y) for y in (0, 3, 1, 2)]

    def first_end(a):
        for r in range(1, 5):
            pads(yp, a, r)
        near = cb[a].reshape(256, C)
        parts = []
        for side, row, dy in ((0, 1, 2), (1, 4, 0)):
            lhs = jnp.concatenate([yp[a, row, 16 * dx : 16 * dx + 256, :] for dx in range(3)], axis=1)
            parts.append(jnp.dot(lhs, cw2[dy].reshape(3 * C, C), preferred_element_type=F32))
        for side in (0, 1):
            parts[side] = parts[side] + jnp.dot(mats[8 + side], near, preferred_element_type=F32)
        for side in (0, 1):
            psend[side, a] = parts[side].astype(BF)

    def send_parts(a):
        @pl.when(has_up)
        def _():
            part_copy(a, True).start()

        @pl.when(has_down)
        def _():
            part_copy(a, False).start()

    with jax.named_scope("load_wait"):
        loads[0].wait()
        loads[1].wait()
        row_load(0).wait()
        row_load(3).wait()
    edge_units = [(f, r) for f in range(FL) for r in (0, 3)]
    with jax.named_scope("norm03"):
        normalize(edge_units, 0, 128)
    norm_copy(0).start()
    norm_copy(1).start()
    with jax.named_scope("norm03b"):
        normalize(edge_units, 128, 128)
    norm_copy(2).start()
    norm_copy(3).start()
    with jax.named_scope("weights"):
        for copy in loads[2:7]:
            copy.wait()
        wqp[...] = jnp.dot(raw[0], mats[1], preferred_element_type=F32).astype(BF)
        wkv[:, 0:256] = jnp.dot(raw[1], mats[1], preferred_element_type=F32).astype(BF)
        wkv[:, 256:512] = jnp.dot(raw[2], mats[1], preferred_element_type=F32).astype(BF)
        wop[...] = jnp.dot(mats[2], raw[3], preferred_element_type=F32).astype(BF)
    with jax.named_scope("keys03"):
        project((0, 3), range(0, 4), True, 0, 128)
    wait_norms((0, 1))
    with jax.named_scope("keys03b"):
        project((0, 3), range(4, 8), False, 0, 128)

    def edge_pair(k, h, beside, meet=False):
        frames = (2 * k, 2 * k + 1)
        attend([(a, r, 128 * h) for a in frames for r in (0, 3)], 128, beside)
        if meet:
            with jax.named_scope("meet"):
                meet_neighbours()
        for a in frames:
            send_edges(a, h)

    with jax.named_scope("attend03"):
        edge_pair(0, 0, [lambda k=k: project((0, 3), (2 * k, 2 * k + 1), True, 128, 128) for k in range(2)], True)
    row_load(1).wait()
    row_load(2).wait()

    def inner_norm(pair, carry):
        normalize([(2 * pair + k, r) for k in range(2) for r in (1, 2)], 0, 256)
        return carry

    with jax.named_scope("norm12"):
        lax.fori_loop(0, 2, inner_norm, 0)
    norm_copy(4).start()
    norm_copy(5).start()
    wait_norms((2, 3))
    with jax.named_scope("attend03b"):
        project((0, 3), range(4, 8), False, 128, 128)
        edge_pair(0, 1, [])
    with jax.named_scope("attend03c"):
        edge_pair(1, 0, [lambda b=b: project((1, 2), (b,), True, 0, 256) for b in range(0, 4)])
    wait_norms((4, 5))
    with jax.named_scope("attend03d"):
        edge_pair(1, 1, [lambda b=b: project((1, 2), (b,), False, 0, 256) for b in range(4, 8)])
    with jax.named_scope("attend12"):
        attend([(0, 1, 0), (0, 2, 0)], 256)
    for copy in loads[7:]:
        copy.wait()

    def mixed_step(a, carry):
        first_wait(a)
        for r in range(6):
            pads(xp, a, r)
        attend([(a + 1, 1, 0), (a + 1, 2, 0)], 256, first_rows(a))
        first_end(a)
        send_parts(a)
        return carry

    with jax.named_scope("mixed"):
        lax.fori_loop(0, FL - 1, mixed_step, 0)
    with jax.named_scope("first"):
        first_wait(FL - 1)
        for r in range(6):
            pads(xp, FL - 1, r)
        for run in first_rows(FL - 1):
            run()
        first_end(FL - 1)
        send_parts(FL - 1)

    def second_step(a, carry):
        near = cb[a].reshape(256, C)
        inner = jnp.dot(taps(yp, a, 1, 2), cw2[...].reshape(9 * C, C), preferred_element_type=F32)
        outer = []
        for row, first, dys in ((0, 1, (1, 2)), (3, 3, (0, 1))):
            parts = [yp[a, first + k, 16 * dx : 16 * dx + 256, :] for k in range(2) for dx in range(3)]
            weight = cw2[dys[0] : dys[0] + 2].reshape(6 * C, C)
            outer.append(jnp.dot(jnp.concatenate(parts, axis=1), weight, preferred_element_type=F32))
        up = jnp.dot(mats[4:8].reshape(4 * 256, 256), near, preferred_element_type=F32)
        for row, value in ((1, inner[0:256]), (2, inner[256:512]), (0, outer[0]), (3, outer[1])):
            value = value + up[256 * row : 256 * row + 256] + fp[a, row].astype(F32)
            if row in (1, 2):
                fp[a, row] = value.astype(BF)
            else:
                acc[a, row // 3] = value
        return carry

    with jax.named_scope("second"):
        lax.fori_loop(0, FL, second_step, 0)

    def edge_part(a, side):
        near = cb[a].reshape(256, C)
        precv[1 - side, a] = jnp.dot(mats[8 + side], near, preferred_element_type=F32).astype(BF)

    def last_step(a, carry):
        @pl.when(has_up)
        def _():
            with jax.named_scope("part_wait_up"):
                part_copy(a, False).wait_recv()

        @pl.when(jnp.logical_not(has_up))
        def _():
            edge_part(a, 0)

        @pl.when(has_down)
        def _():
            with jax.named_scope("part_wait_down"):
                part_copy(a, True).wait_recv()

        @pl.when(jnp.logical_not(has_down))
        def _():
            edge_part(a, 1)

        for row, side in ((0, 1), (3, 0)):
            value = (acc[a, row // 3] + precv[side, a].astype(F32)).astype(BF)
            ob[a, row] = jnp.dot(mats[0], value, preferred_element_type=F32).astype(BF)
        return carry

    def restore_step(a, carry):
        for row in (1, 2):
            ob[a, row] = jnp.dot(mats[0], fp[a, row], preferred_element_type=F32).astype(BF)
        return carry

    with jax.named_scope("restore"):
        lax.fori_loop(0, FL, restore_step, 0)
    with jax.named_scope("last"):
        lax.fori_loop(0, FL, last_step, 0)

    def drain(a, carry):

        @pl.when(has_up)
        def _():
            for h in range(2):
                edge_copy(a, True, h).wait_send()
            part_copy(a, True).wait_send()

        @pl.when(has_down)
        def _():
            for h in range(2):
                edge_copy(a, False, h).wait_send()
            part_copy(a, False).wait_send()

        return carry

    for k in range(6):
        norm_copy(k).wait_send()
    with jax.named_scope("drain"):
        lax.fori_loop(0, FL, drain, 0)


def solution(mesh):
    spaces = mesh.shape["space"]
    constants = tables()
    place = positions()

    def local(fine, coarse, w_query, w_key, w_value, w_out, conv_first, conv_second):
        anywhere = pl.BlockSpec(memory_space=pl.ANY)
        dma = pltpu.SemaphoreType.DMA
        shape = (FL, RL, W, C)
        mats = jnp.asarray(constants)
        moved = pl.pallas_call(
            lambda *refs: kernel(spaces, *refs),
            out_shape=pltpu.VMEM(shape, BF),
            in_specs=[anywhere] * 10,
            out_specs=pl.BlockSpec(memory_space=pltpu.VMEM),
            scratch_shapes=[
                pltpu.VMEM(shape, BF),
                pltpu.VMEM((FL, 2, 128, C), BF),
                pltpu.VMEM((4, C, C), BF),
                pltpu.VMEM((10, 256, 256), BF),
                pltpu.VMEM((8, 1, C), F32),
                pltpu.VMEM((3, 3, C, C), BF),
                pltpu.VMEM((3, 3, C, C), BF),
                pltpu.VMEM((C, C), BF),
                pltpu.VMEM((C, 2 * C), BF),
                pltpu.VMEM((C, C), BF),
                pltpu.VMEM((2 * FL, RL, W, C), BF),
                pltpu.VMEM(shape, BF),
                pltpu.VMEM((RL, FL, W, C), BF),
                pltpu.VMEM((RL, 2 * FL, W, C), BF),
                pltpu.VMEM((RL, 2 * FL, W, C), BF),
                pltpu.VMEM((2 * W, C), BF),
                pltpu.VMEM((FL, RL + 2, W + 32, C), BF),
                pltpu.VMEM((FL, RL + 2, W + 32, C), BF),
                pltpu.VMEM((FL, 2, W, C), F32),
                pltpu.VMEM((2, FL, W, C), BF),
                pltpu.VMEM((2, FL, W, C), BF),
                dma((10,)),
                dma((RL,)),
                dma((6,)),
                dma((6,)),
                dma((2, FL, 2)),
                dma((2, FL, 2)),
                dma((2, FL)),
                dma((2, FL)),
                pltpu.SemaphoreType.REGULAR,
                pltpu.SemaphoreType.REGULAR,
            ],
            compiler_params=pltpu.CompilerParams(
                collective_id=0, has_side_effects=True, vmem_limit_bytes=60 * 1024 * 1024),
            name="fused",
        )(fine, coarse, w_query, w_key, w_value, w_out, conv_first, conv_second, mats, jnp.asarray(place))
        def emit(x, o, sem):
            copy = pltpu.make_async_copy(x, o, sem)
            copy.start()
            copy.wait()

        return pl.pallas_call(
            emit,
            out_shape=jax.ShapeDtypeStruct(shape, BF),
            in_specs=[pl.BlockSpec(memory_space=pltpu.VMEM)],
            out_specs=anywhere,
            scratch_shapes=[dma],
            name="emit",
        )(pltpu.with_memory_space_constraint(moved, pltpu.VMEM))

    return jax.shard_map(
        local,
        mesh=mesh,
        in_specs=(P("tm", "space", None, None), P("tm", "space", None, None), P(), P(), P(), P(), P(), P()),
        out_specs=P("tm", "space", None, None),
        check_vma=False,
    )
```

time: 38.3 us -> 36.4 us (0.950)
  Pallas kernels: 38.2 us -> 36.2 us
    pallas_call x1, Pallas kernels: 36.9 us -> 34.8 us  [local(): pl.pallas_call(lambda *refs: kernel(spaces, *refs), out_shape=pltpu.VMEM(...]
where the time goes in v2:
time: 36.4 us; the launch traced here: 36.3 us
  Pallas kernels  36.2 us (99%)
    pallas_call x1, Pallas kernels, local(): pl.pallas_call(lambda *refs: kernel(spaces, *refs), out_shape=pltpu.VMEM(...  34.8 us
    pallas_call x1, Pallas kernels, local(): pl.pallas_call(emit, out_shape=jax.ShapeDtypeStruct(shape, BF), in_specs=...  1.33 us

profile of v2, /device:TPU:96, one launch (start us, length us, event | category | flops | bytes accessed | tf_op | source)
XLA Modules:
  0.0 36.3 jit_solution(1806033254902005334)
XLA Ops:
  0.0 34.8 %fused.1.x = bf16[4,4,256,256]{3,2,1,0:T(8,128)(2,1)S(1)} custom-call(bf16[4,4,256,256]{3,2,1,0:T(8,128)(2,1)} %refs_0_.1, bf16[4,2,128,256]{3,2,1,0:T(8,128)(2,1)} %refs_1_.1, bf16[256,256]{1,0:T(8,128)(2,1)} %refs_2_.1, bf16[256,256]{1,0:T(8,128)(2,1)} %refs_3_.1, bf16[256,256]{1,0:T(8,128)(2,1)} %refs_4_.1, bf16[256,256]{1,0:T(8,128)(2,1)} %refs_5_.1, ...), custom_call_target="tpu_custom_call" | custom-call | tf_op jit(solution)/shard_map/fused/pallas_call | solution.py:488
  34.8 1.3 %emit.1 = bf16[4,4,256,256]{3,2,1,0:T(8,128)(2,1)} custom-call(bf16[4,4,256,256]{3,2,1,0:T(8,128)(2,1)S(1)} %fused.1.x), custom_call_target="tpu_custom_call" | custom-call | tf_op jit(solution)/shard_map/emit/pallas_call | solution.py:535

commit v3 on v2

--- a/solution.py
+++ b/solution.py
@@ -83,19 +83,18 @@
         return pltpu.make_async_copy(fine_hbm.at[:, r], fin.at[:, r], row_sem.at[r])
 
     loads = [
-        pltpu.make_async_copy(mats_hbm.at[0], mats.at[0], load_sem.at[0]),
-        pltpu.make_async_copy(pos_hbm, pos, load_sem.at[1]),
-        pltpu.make_async_copy(wq_hbm, raw.at[0], load_sem.at[2]),
-        pltpu.make_async_copy(wk_hbm, raw.at[1], load_sem.at[3]),
-        pltpu.make_async_copy(wv_hbm, raw.at[2], load_sem.at[4]),
-        pltpu.make_async_copy(wo_hbm, raw.at[3], load_sem.at[5]),
-        pltpu.make_async_copy(mats_hbm.at[pl.ds(1, 9)], mats.at[pl.ds(1, 9)], load_sem.at[9]),
-        pltpu.make_async_copy(coarse_hbm, cb, load_sem.at[6]),
-        pltpu.make_async_copy(c1_hbm, cw1, load_sem.at[7]),
-        pltpu.make_async_copy(c2_hbm, cw2, load_sem.at[8]),
+        pltpu.make_async_copy(mats_hbm.at[pl.ds(0, 3)], mats.at[pl.ds(0, 3)], load_sem.at[0]),
+        pltpu.make_async_copy(mats_hbm.at[pl.ds(0, 4)], raw, load_sem.at[1]),
+        pltpu.make_async_copy(pos_hbm, pos, load_sem.at[2]),
+        pltpu.make_async_copy(mats_hbm.at[pl.ds(3, 7)], mats.at[pl.ds(3, 7)], load_sem.at[3]),
+        pltpu.make_async_copy(coarse_hbm, cb, load_sem.at[4]),
+        pltpu.make_async_copy(c1_hbm, cw1, load_sem.at[5]),
+        pltpu.make_async_copy(c2_hbm, cw2, load_sem.at[6]),
     ]
     loads[0].start()
-    loads[1].start()
+    for k, weight in enumerate((wq_hbm, wk_hbm, wv_hbm, wo_hbm)):
+        pltpu.make_async_copy(weight, raw.at[k], load_sem.at[1]).start()
+    loads[2].start()
     row_load(0).start()
     row_load(3).start()
 
@@ -105,11 +104,10 @@
     def _():
         pl.semaphore_signal(barrier, inc=1, device_id=(1 - t, s), device_id_type=MESH)
 
-    for copy in loads[2:7]:
-        copy.start()
+    loads[3].start()
     row_load(1).start()
     row_load(2).start()
-    for copy in loads[7:]:
+    for copy in loads[4:]:
         copy.start()
 
     @pl.when(t == 0)
@@ -128,16 +126,6 @@
     @pl.when(jnp.logical_and(t == 1, has_down))
     def _():
         pl.semaphore_signal(barrier, inc=1, device_id=(t, s + 1), device_id_type=MESH)
-
-    def meet_neighbours():
-        @pl.when(t == 1)
-        def _():
-            pl.semaphore_wait(barrier, has_up.astype(jnp.int32) + has_down.astype(jnp.int32))
-            pl.semaphore_signal(far_sem, inc=1, device_id=(1 - t, s), device_id_type=MESH)
-
-        @pl.when(t == 0)
-        def _():
-            pl.semaphore_wait(far_sem, 1)
 
     zero_row = jnp.zeros((FL, 288, C), BF)
 
@@ -154,7 +142,7 @@
         px = pl.ds((0, 0, 128, 128, 0, 0)[k], 128 if k < 4 else 256)
         return pltpu.make_async_remote_copy(
             src_ref=nbuf.at[pl.ds(0, FL), r, px], dst_ref=nbuf.at[pl.ds(FL, FL), r, px],
-            send_sem=nsend.at[k], recv_sem=nrecv.at[k],
+            send_sem=nsend, recv_sem=nrecv.at[k],
             device_id=(1 - t, s), device_id_type=MESH)
 
     def normalize(units, start, count):
@@ -173,7 +161,7 @@
         px = pl.ds(16 + 128 * h, 128)
         return pltpu.make_async_remote_copy(
             src_ref=xp.at[a, row, px], dst_ref=xp.at[a, slot, px],
-            send_sem=xsend.at[side, a, h], recv_sem=xrecv.at[side, a, h],
+            send_sem=xsend.at[side], recv_sem=xrecv.at[side, a, h],
             device_id=(t, to), device_id_type=MESH)
 
     def part_copy(a, up):
@@ -181,7 +169,7 @@
         to = s - 1 if up else s + 1
         return pltpu.make_async_remote_copy(
             src_ref=psend.at[side, a], dst_ref=precv.at[side, a],
-            send_sem=tsend.at[side, a], recv_sem=trecv.at[side, a],
+            send_sem=tsend.at[side], recv_sem=trecv.at[side, a],
             device_id=(t, to), device_id_type=MESH)
 
     factor = float(np.log2(np.e) / np.sqrt(32.0))
@@ -247,21 +235,26 @@
                     beside.pop(0)()
         for run in beside:
             run()
-        branch = jnp.dot(att[...], wop[...], preferred_element_type=F32)
+        branch = jnp.dot(att[0:into], wop[...], preferred_element_type=F32)
         for i, (a, r, start) in enumerate(units):
             px = slice(start, start + count)
             moved = (fp[a, r, px].astype(F32) + branch[count * i : count * i + count]).astype(BF)
             fp[a, r, px] = moved
             xp[a, r + 1, 16 + start : 16 + start + count, :] = jnp.maximum(moved, jnp.zeros_like(moved))
 
+    def send_up(a, h):
+        @pl.when(has_up)
+        def _():
+            edge_copy(a, True, h).start()
+
+    def send_down(a, h):
+        @pl.when(has_down)
+        def _():
+            edge_copy(a, False, h).start()
+
     def send_edges(a, h):
-        @pl.when(has_up)
-        def _():
-            edge_copy(a, True, h).start()
-
-        @pl.when(has_down)
-        def _():
-            edge_copy(a, False, h).start()
+        send_down(a, h)
+        send_up(a, h)
 
     def wait_norms(ks):
         with jax.named_scope("norm_wait"):
@@ -281,14 +274,14 @@
                 for h in range(2):
                     edge_copy(a, True, h).wait_recv()
 
-    def first_rows(a):
+    def first_rows(a, rows):
         weight = cw1[...].reshape(9 * C, C)
 
         def run(y):
             result = jnp.dot(taps(xp, a, y, 1), weight, preferred_element_type=F32)
             yp[a, 1 + y, 16:272, :] = jnp.maximum(result, 0.0).astype(BF)
 
-        return [lambda y=y: run(y) for y in (0, 3, 1, 2)]
+        return [lambda y=y: run(y) for y in rows]
 
     def first_end(a):
         for r in range(1, 5):
@@ -312,9 +305,15 @@
         def _():
             part_copy(a, False).start()
 
+    with jax.named_scope("weights"):
+        for copy in loads[:2]:
+            copy.wait()
+        wqp[...] = jnp.dot(raw[0], mats[1], preferred_element_type=F32).astype(BF)
+        wkv[:, 0:256] = jnp.dot(raw[1], mats[1], preferred_element_type=F32).astype(BF)
+        wkv[:, 256:512] = jnp.dot(raw[2], mats[1], preferred_element_type=F32).astype(BF)
+        wop[...] = jnp.dot(mats[2], raw[3], preferred_element_type=F32).astype(BF)
     with jax.named_scope("load_wait"):
-        loads[0].wait()
-        loads[1].wait()
+        loads[2].wait()
         row_load(0).wait()
         row_load(3).wait()
     edge_units = [(f, r) for f in range(FL) for r in (0, 3)]
@@ -326,74 +325,92 @@
         normalize(edge_units, 128, 128)
     norm_copy(2).start()
     norm_copy(3).start()
-    with jax.named_scope("weights"):
-        for copy in loads[2:7]:
-            copy.wait()
-        wqp[...] = jnp.dot(raw[0], mats[1], preferred_element_type=F32).astype(BF)
-        wkv[:, 0:256] = jnp.dot(raw[1], mats[1], preferred_element_type=F32).astype(BF)
-        wkv[:, 256:512] = jnp.dot(raw[2], mats[1], preferred_element_type=F32).astype(BF)
-        wop[...] = jnp.dot(mats[2], raw[3], preferred_element_type=F32).astype(BF)
     with jax.named_scope("keys03"):
         project((0, 3), range(0, 4), True, 0, 128)
     wait_norms((0, 1))
     with jax.named_scope("keys03b"):
         project((0, 3), range(4, 8), False, 0, 128)
 
-    def edge_pair(k, h, beside, meet=False):
+    def edge_pair(k, h, beside):
         frames = (2 * k, 2 * k + 1)
         attend([(a, r, 128 * h) for a in frames for r in (0, 3)], 128, beside)
-        if meet:
-            with jax.named_scope("meet"):
-                meet_neighbours()
         for a in frames:
             send_edges(a, h)
 
+    loads[3].wait()
+
+    @pl.when(t == 1)
+    def _():
+        pl.semaphore_wait(barrier, has_up.astype(jnp.int32) + has_down.astype(jnp.int32))
+        pl.semaphore_signal(far_sem, inc=1, device_id=(1 - t, s), device_id_type=MESH)
+
     with jax.named_scope("attend03"):
-        edge_pair(0, 0, [lambda k=k: project((0, 3), (2 * k, 2 * k + 1), True, 128, 128) for k in range(2)], True)
-    row_load(1).wait()
-    row_load(2).wait()
-
+        attend([(0, 3, 0)], 128)
+        with jax.named_scope("meet"):
+            @pl.when(t == 0)
+            def _():
+                pl.semaphore_wait(far_sem, 1)
+
+        send_down(0, 0)
+        attend([(0, 0, 0)], 128)
+        send_up(0, 0)
+        attend([(1, 0, 0), (1, 3, 0)], 128, [lambda k=k: project((0, 3), (2 * k, 2 * k + 1), True, 128, 128) for k in range(2)])
+        send_edges(1, 0)
     def inner_norm(pair, carry):
         normalize([(2 * pair + k, r) for k in range(2) for r in (1, 2)], 0, 256)
         return carry
 
-    with jax.named_scope("norm12"):
-        lax.fori_loop(0, 2, inner_norm, 0)
-    norm_copy(4).start()
-    norm_copy(5).start()
     wait_norms((2, 3))
     with jax.named_scope("attend03b"):
         project((0, 3), range(4, 8), False, 128, 128)
         edge_pair(0, 1, [])
+    with jax.named_scope("norm12"):
+        row_load(1).wait()
+        row_load(2).wait()
+        lax.fori_loop(0, 2, inner_norm, 0)
+    norm_copy(4).start()
+    norm_copy(5).start()
     with jax.named_scope("attend03c"):
         edge_pair(1, 0, [lambda b=b: project((1, 2), (b,), True, 0, 256) for b in range(0, 4)])
+    with jax.named_scope("attend03d"):
+        edge_pair(1, 1, [])
     wait_norms((4, 5))
-    with jax.named_scope("attend03d"):
-        edge_pair(1, 1, [lambda b=b: project((1, 2), (b,), False, 0, 256) for b in range(4, 8)])
+    with jax.named_scope("keys12b"):
+        for b in range(4, 8, 2):
+            project((1, 2), (b, b + 1), False, 0, 256)
     with jax.named_scope("attend12"):
         attend([(0, 1, 0), (0, 2, 0)], 256)
-    for copy in loads[7:]:
+    for copy in loads[4:]:
         copy.wait()
 
     def mixed_step(a, carry):
+        for r in range(1, 5):
+            pads(xp, a, r)
+        attend([(a + 1, 1, 0), (a + 1, 2, 0)], 256, first_rows(a, (1, 2)))
         first_wait(a)
-        for r in range(6):
-            pads(xp, a, r)
-        attend([(a + 1, 1, 0), (a + 1, 2, 0)], 256, first_rows(a))
-        first_end(a)
+        outer(a)
         send_parts(a)
         return carry
+
+    def outer(a):
+        for r in (0, 5):
+            pads(xp, a, r)
+        for run in first_rows(a, (0, 3)):
+            run()
+        first_end(a)
 
     with jax.named_scope("mixed"):
         lax.fori_loop(0, FL - 1, mixed_step, 0)
     with jax.named_scope("first"):
+        for r in range(1, 5):
+            pads(xp, FL - 1, r)
         first_wait(FL - 1)
-        for r in range(6):
-            pads(xp, FL - 1, r)
-        for run in first_rows(FL - 1):
+        outer(FL - 1)
+        send_parts(FL - 1)
+        for run in first_rows(FL - 1, (1, 2)):
             run()
-        first_end(FL - 1)
-        send_parts(FL - 1)
+        for r in (2, 3):
+            pads(yp, FL - 1, r)
 
     def second_step(a, carry):
         near = cb[a].reshape(256, C)
@@ -453,26 +470,21 @@
     with jax.named_scope("last"):
         lax.fori_loop(0, FL, last_step, 0)
 
-    def drain(a, carry):
-
-        @pl.when(has_up)
-        def _():
-            for h in range(2):
-                edge_copy(a, True, h).wait_send()
-            part_copy(a, True).wait_send()
-
-        @pl.when(has_down)
-        def _():
-            for h in range(2):
-                edge_copy(a, False, h).wait_send()
-            part_copy(a, False).wait_send()
-
-        return carry
-
-    for k in range(6):
-        norm_copy(k).wait_send()
     with jax.named_scope("drain"):
-        lax.fori_loop(0, FL, drain, 0)
+        pltpu.make_async_remote_copy(
+            src_ref=nbuf.at[pl.ds(0, FL)], dst_ref=nbuf.at[pl.ds(FL, FL)], send_sem=nsend, recv_sem=nrecv.at[0],
+            device_id=(1 - t, s), device_id_type=MESH).wait_send()
+        for side, flag, row, slot, to in ((0, has_up, 1, 5, s - 1), (1, has_down, 4, 0, s + 1)):
+            @pl.when(flag)
+            def _(side=side, row=row, slot=slot, to=to):
+                pltpu.make_async_remote_copy(
+                    src_ref=xp.at[:, row, pl.ds(16, 256)], dst_ref=xp.at[:, slot, pl.ds(16, 256)],
+                    send_sem=xsend.at[side], recv_sem=xrecv.at[side, 0, 0],
+                    device_id=(t, to), device_id_type=MESH).wait_send()
+                pltpu.make_async_remote_copy(
+                    src_ref=psend.at[side], dst_ref=precv.at[side],
+                    send_sem=tsend.at[side], recv_sem=trecv.at[side, 0],
+                    device_id=(t, to), device_id_type=MESH).wait_send()
 
 
 def solution(mesh):
@@ -512,13 +524,13 @@
                 pltpu.VMEM((FL, 2, W, C), F32),
                 pltpu.VMEM((2, FL, W, C), BF),
                 pltpu.VMEM((2, FL, W, C), BF),
-                dma((10,)),
+                dma((7,)),
                 dma((RL,)),
+                dma,
                 dma((6,)),
-                dma((6,)),
+                dma((2,)),
                 dma((2, FL, 2)),
-                dma((2, FL, 2)),
-                dma((2, FL)),
+                dma((2,)),
                 dma((2, FL)),
                 pltpu.SemaphoreType.REGULAR,
                 pltpu.SemaphoreType.REGULAR,
@@ -528,9 +540,10 @@
             name="fused",
         )(fine, coarse, w_query, w_key, w_value, w_out, conv_first, conv_second, mats, jnp.asarray(place))
         def emit(x, o, sem):
-            copy = pltpu.make_async_copy(x, o, sem)
-            copy.start()
-            copy.wait()
+            for f in range(FL):
+                for r in range(0, RL, 2):
+                    pltpu.make_async_copy(x.at[f, pl.ds(r, 2)], o.at[f, pl.ds(r, 2)], sem).start()
+            pltpu.make_async_copy(x, o, sem).wait()
 
         return pl.pallas_call(
             emit,

time: 36.4 us -> 35.9 us (0.986)
  Pallas kernels: 36.2 us -> 35.4 us
    pallas_call x1, Pallas kernels: 34.8 us -> 34.1 us  [local(): pl.pallas_call(lambda *refs: kernel(spaces, *refs), out_shape=pltpu.VMEM(...]
where the time goes in v3:
time: 35.9 us; the launch traced here: 35.6 us
  Pallas kernels  35.4 us (99%)
    pallas_call x1, Pallas kernels, local(): pl.pallas_call(lambda *refs: kernel(spaces, *refs), out_shape=pltpu.VMEM(...  34.1 us
    pallas_call x1, Pallas kernels, local(): pl.pallas_call(emit, out_shape=jax.ShapeDtypeStruct(shape, BF), in_specs=...  1.31 us

profile of v3, /device:TPU:96, one launch (start us, length us, event | category | flops | bytes accessed | tf_op | source)
XLA Modules:
  0.0 35.6 jit_solution(10287495767082732288)
XLA Ops:
  0.0 34.1 %fused.1.x = bf16[4,4,256,256]{3,2,1,0:T(8,128)(2,1)S(1)} custom-call(bf16[4,4,256,256]{3,2,1,0:T(8,128)(2,1)} %refs_0_.1, bf16[4,2,128,256]{3,2,1,0:T(8,128)(2,1)} %refs_1_.1, bf16[256,256]{1,0:T(8,128)(2,1)} %refs_2_.1, bf16[256,256]{1,0:T(8,128)(2,1)} %refs_3_.1, bf16[256,256]{1,0:T(8,128)(2,1)} %refs_4_.1, bf16[256,256]{1,0:T(8,128)(2,1)} %refs_5_.1, ...), custom_call_target="tpu_custom_call" | custom-call | tf_op jit(solution)/shard_map/fused/pallas_call | solution.py:500
  34.1 1.3 %emit.1 = bf16[4,4,256,256]{3,2,1,0:T(8,128)(2,1)} custom-call(bf16[4,4,256,256]{3,2,1,0:T(8,128)(2,1)S(1)} %fused.1.x), custom_call_target="tpu_custom_call" | custom-call | tf_op jit(solution)/shard_map/emit/pallas_call | solution.py:548

commit v4 on v3

--- a/solution.py
+++ b/solution.py
@@ -83,20 +83,23 @@
         return pltpu.make_async_copy(fine_hbm.at[:, r], fin.at[:, r], row_sem.at[r])
 
     loads = [
-        pltpu.make_async_copy(mats_hbm.at[pl.ds(0, 3)], mats.at[pl.ds(0, 3)], load_sem.at[0]),
+        pltpu.make_async_copy(mats_hbm.at[0], mats.at[0], load_sem.at[0]),
         pltpu.make_async_copy(mats_hbm.at[pl.ds(0, 4)], raw, load_sem.at[1]),
         pltpu.make_async_copy(pos_hbm, pos, load_sem.at[2]),
-        pltpu.make_async_copy(mats_hbm.at[pl.ds(3, 7)], mats.at[pl.ds(3, 7)], load_sem.at[3]),
+        pltpu.make_async_copy(mats_hbm.at[pl.ds(1, 2)], mats.at[pl.ds(1, 2)], load_sem.at[3]),
         pltpu.make_async_copy(coarse_hbm, cb, load_sem.at[4]),
         pltpu.make_async_copy(c1_hbm, cw1, load_sem.at[5]),
         pltpu.make_async_copy(c2_hbm, cw2, load_sem.at[6]),
+        pltpu.make_async_copy(mats_hbm.at[pl.ds(3, 7)], mats.at[pl.ds(3, 7)], load_sem.at[7]),
     ]
+    for r in (3, 0):
+        for f in range(FL):
+            pltpu.make_async_copy(fine_hbm.at[f, r], fin.at[f, r], row_sem.at[r]).start()
     loads[0].start()
+    loads[2].start()
     for k, weight in enumerate((wq_hbm, wk_hbm, wv_hbm, wo_hbm)):
         pltpu.make_async_copy(weight, raw.at[k], load_sem.at[1]).start()
-    loads[2].start()
-    row_load(0).start()
-    row_load(3).start()
+    loads[3].start()
 
     barrier = pltpu.get_barrier_semaphore()
 
@@ -104,11 +107,6 @@
     def _():
         pl.semaphore_signal(barrier, inc=1, device_id=(1 - t, s), device_id_type=MESH)
 
-    loads[3].start()
-    row_load(1).start()
-    row_load(2).start()
-    for copy in loads[4:]:
-        copy.start()
 
     @pl.when(t == 0)
     def _():
@@ -305,31 +303,34 @@
         def _():
             part_copy(a, False).start()
 
+    with jax.named_scope("load_wait"):
+        loads[0].wait()
+        loads[2].wait()
+        row_load(0).wait()
+        row_load(3).wait()
+    loads[7].start()
+    row_load(1).start()
+    row_load(2).start()
+    for copy in loads[4:7]:
+        copy.start()
+    edge_units = [(f, r) for f in range(FL) for r in (0, 3)]
+    with jax.named_scope("norm03"):
+        normalize(edge_units, 0, 128)
+    norm_copy(1).start()
+    norm_copy(0).start()
     with jax.named_scope("weights"):
-        for copy in loads[:2]:
-            copy.wait()
+        loads[1].wait()
+        loads[3].wait()
         wqp[...] = jnp.dot(raw[0], mats[1], preferred_element_type=F32).astype(BF)
         wkv[:, 0:256] = jnp.dot(raw[1], mats[1], preferred_element_type=F32).astype(BF)
         wkv[:, 256:512] = jnp.dot(raw[2], mats[1], preferred_element_type=F32).astype(BF)
         wop[...] = jnp.dot(mats[2], raw[3], preferred_element_type=F32).astype(BF)
-    with jax.named_scope("load_wait"):
-        loads[2].wait()
-        row_load(0).wait()
-        row_load(3).wait()
-    edge_units = [(f, r) for f in range(FL) for r in (0, 3)]
-    with jax.named_scope("norm03"):
-        normalize(edge_units, 0, 128)
-    norm_copy(0).start()
-    norm_copy(1).start()
+    with jax.named_scope("keys03"):
+        project((0, 3), range(0, 4), True, 0, 128)
     with jax.named_scope("norm03b"):
         normalize(edge_units, 128, 128)
+    norm_copy(3).start()
     norm_copy(2).start()
-    norm_copy(3).start()
-    with jax.named_scope("keys03"):
-        project((0, 3), range(0, 4), True, 0, 128)
-    wait_norms((0, 1))
-    with jax.named_scope("keys03b"):
-        project((0, 3), range(4, 8), False, 0, 128)
 
     def edge_pair(k, h, beside):
         frames = (2 * k, 2 * k + 1)
@@ -337,14 +338,15 @@
         for a in frames:
             send_edges(a, h)
 
-    loads[3].wait()
-
     @pl.when(t == 1)
     def _():
         pl.semaphore_wait(barrier, has_up.astype(jnp.int32) + has_down.astype(jnp.int32))
         pl.semaphore_signal(far_sem, inc=1, device_id=(1 - t, s), device_id_type=MESH)
 
     with jax.named_scope("attend03"):
+        loads[7].wait()
+        wait_norms((1,))
+        project((3,), range(4, 8), False, 0, 128)
         attend([(0, 3, 0)], 128)
         with jax.named_scope("meet"):
             @pl.when(t == 0)
@@ -352,6 +354,8 @@
                 pl.semaphore_wait(far_sem, 1)
 
         send_down(0, 0)
+        wait_norms((0,))
+        project((0,), range(4, 8), False, 0, 128)
         attend([(0, 0, 0)], 128)
         send_up(0, 0)
         attend([(1, 0, 0), (1, 3, 0)], 128, [lambda k=k: project((0, 3), (2 * k, 2 * k + 1), True, 128, 128) for k in range(2)])
@@ -380,7 +384,7 @@
             project((1, 2), (b, b + 1), False, 0, 256)
     with jax.named_scope("attend12"):
         attend([(0, 1, 0), (0, 2, 0)], 256)
-    for copy in loads[4:]:
+    for copy in loads[4:7]:
         copy.wait()
 
     def mixed_step(a, carry):
@@ -524,7 +528,7 @@
                 pltpu.VMEM((FL, 2, W, C), F32),
                 pltpu.VMEM((2, FL, W, C), BF),
                 pltpu.VMEM((2, FL, W, C), BF),
-                dma((7,)),
+                dma((8,)),
                 dma((RL,)),
                 dma,
                 dma((6,)),

time: 35.9 us -> 35.3 us (0.983)
  Pallas kernels: 35.4 us -> 34.9 us
    pallas_call x1, Pallas kernels: 34.1 us -> 33.6 us  [local(): pl.pallas_call(lambda *refs: kernel(spaces, *refs), out_shape=pltpu.VMEM(...]
where the time goes in v4:
time: 35.3 us; the launch traced here: 35.1 us
  Pallas kernels  34.9 us (99%)
    pallas_call x1, Pallas kernels, local(): pl.pallas_call(lambda *refs: kernel(spaces, *refs), out_shape=pltpu.VMEM(...  33.6 us
    pallas_call x1, Pallas kernels, local(): pl.pallas_call(emit, out_shape=jax.ShapeDtypeStruct(shape, BF), in_specs=...  1.31 us

profile of v4, /device:TPU:96, one launch (start us, length us, event | category | flops | bytes accessed | tf_op | source)
XLA Modules:
  0.0 35.1 jit_solution(7886702773207536252)
XLA Ops:
  0.0 33.6 %fused.1.x = bf16[4,4,256,256]{3,2,1,0:T(8,128)(2,1)S(1)} custom-call(bf16[4,4,256,256]{3,2,1,0:T(8,128)(2,1)} %refs_0_.1, bf16[4,2,128,256]{3,2,1,0:T(8,128)(2,1)} %refs_1_.1, bf16[256,256]{1,0:T(8,128)(2,1)} %refs_2_.1, bf16[256,256]{1,0:T(8,128)(2,1)} %refs_3_.1, bf16[256,256]{1,0:T(8,128)(2,1)} %refs_4_.1, bf16[256,256]{1,0:T(8,128)(2,1)} %refs_5_.1, ...), custom_call_target="tpu_custom_call" | custom-call | tf_op jit(solution)/shard_map/fused/pallas_call | solution.py:504
  33.6 1.3 %emit.1 = bf16[4,4,256,256]{3,2,1,0:T(8,128)(2,1)} custom-call(bf16[4,4,256,256]{3,2,1,0:T(8,128)(2,1)S(1)} %fused.1.x), custom_call_target="tpu_custom_call" | custom-call | tf_op jit(solution)/shard_map/emit/pallas_call | solution.py:552

commit v5 on v4

--- a/solution.py
+++ b/solution.py
@@ -79,8 +79,8 @@
     has_up = s > 0
     has_down = s < spaces - 1
 
-    def row_load(r):
-        return pltpu.make_async_copy(fine_hbm.at[:, r], fin.at[:, r], row_sem.at[r])
+    def rows_load(k):
+        return pltpu.make_async_copy(fine_hbm.at[:, pl.ds(1, 2)], fin.at[:, pl.ds(1, 2)], row_sem.at[k])
 
     loads = [
         pltpu.make_async_copy(mats_hbm.at[0], mats.at[0], load_sem.at[0]),
@@ -94,7 +94,7 @@
     ]
     for r in (3, 0):
         for f in range(FL):
-            pltpu.make_async_copy(fine_hbm.at[f, r], fin.at[f, r], row_sem.at[r]).start()
+            pltpu.make_async_copy(fine_hbm.at[f, r], fin.at[f, r], row_sem.at[0]).start()
     loads[0].start()
     loads[2].start()
     for k, weight in enumerate((wq_hbm, wk_hbm, wv_hbm, wo_hbm)):
@@ -159,7 +159,7 @@
         px = pl.ds(16 + 128 * h, 128)
         return pltpu.make_async_remote_copy(
             src_ref=xp.at[a, row, px], dst_ref=xp.at[a, slot, px],
-            send_sem=xsend.at[side], recv_sem=xrecv.at[side, a, h],
+            send_sem=xsend.at[side], recv_sem=xrecv.at[side, a],
             device_id=(t, to), device_id_type=MESH)
 
     def part_copy(a, up):
@@ -259,18 +259,24 @@
             for k in ks:
                 norm_copy(k).wait_recv()
 
+    def edge_whole(a, up):
+        row, slot, to = (1, 5, s - 1) if up else (4, 0, s + 1)
+        side = 0 if up else 1
+        return pltpu.make_async_remote_copy(
+            src_ref=xp.at[a, row, pl.ds(16, 256)], dst_ref=xp.at[a, slot, pl.ds(16, 256)],
+            send_sem=xsend.at[side], recv_sem=xrecv.at[side, a],
+            device_id=(t, to), device_id_type=MESH)
+
     def first_wait(a):
         @pl.when(has_up)
         def _():
             with jax.named_scope("edge_wait_up"):
-                for h in range(2):
-                    edge_copy(a, False, h).wait_recv()
+                edge_whole(a, False).wait_recv()
 
         @pl.when(has_down)
         def _():
             with jax.named_scope("edge_wait_down"):
-                for h in range(2):
-                    edge_copy(a, True, h).wait_recv()
+                edge_whole(a, True).wait_recv()
 
     def first_rows(a, rows):
         weight = cw1[...].reshape(9 * C, C)
@@ -306,11 +312,9 @@
     with jax.named_scope("load_wait"):
         loads[0].wait()
         loads[2].wait()
-        row_load(0).wait()
-        row_load(3).wait()
+        rows_load(0).wait()
     loads[7].start()
-    row_load(1).start()
-    row_load(2).start()
+    rows_load(1).start()
     for copy in loads[4:7]:
         copy.start()
     edge_units = [(f, r) for f in range(FL) for r in (0, 3)]
@@ -369,8 +373,7 @@
         project((0, 3), range(4, 8), False, 128, 128)
         edge_pair(0, 1, [])
     with jax.named_scope("norm12"):
-        row_load(1).wait()
-        row_load(2).wait()
+        rows_load(1).wait()
         lax.fori_loop(0, 2, inner_norm, 0)
     norm_copy(4).start()
     norm_copy(5).start()
@@ -440,7 +443,22 @@
         near = cb[a].reshape(256, C)
         precv[1 - side, a] = jnp.dot(mats[8 + side], near, preferred_element_type=F32).astype(BF)
 
+    def last_row(a, k):
+        value = (acc[a, k] + precv[1 - k, a].astype(F32)).astype(BF)
+        ob[a, 3 * k] = jnp.dot(mats[0], value, preferred_element_type=F32).astype(BF)
+
     def last_step(a, carry):
+        @pl.when(has_down)
+        def _():
+            with jax.named_scope("part_wait_down"):
+                part_copy(a, True).wait_recv()
+
+        @pl.when(jnp.logical_not(has_down))
+        def _():
+            edge_part(a, 1)
+
+        last_row(a, 1)
+
         @pl.when(has_up)
         def _():
             with jax.named_scope("part_wait_up"):
@@ -450,18 +468,7 @@
         def _():
             edge_part(a, 0)
 
-        @pl.when(has_down)
-        def _():
-            with jax.named_scope("part_wait_down"):
-                part_copy(a, True).wait_recv()
-
-        @pl.when(jnp.logical_not(has_down))
-        def _():
-            edge_part(a, 1)
-
-        for row, side in ((0, 1), (3, 0)):
-            value = (acc[a, row // 3] + precv[side, a].astype(F32)).astype(BF)
-            ob[a, row] = jnp.dot(mats[0], value, preferred_element_type=F32).astype(BF)
+        last_row(a, 0)
         return carry
 
     def restore_step(a, carry):
@@ -483,7 +490,7 @@
             def _(side=side, row=row, slot=slot, to=to):
                 pltpu.make_async_remote_copy(
                     src_ref=xp.at[:, row, pl.ds(16, 256)], dst_ref=xp.at[:, slot, pl.ds(16, 256)],
-                    send_sem=xsend.at[side], recv_sem=xrecv.at[side, 0, 0],
+                    send_sem=xsend.at[side], recv_sem=xrecv.at[side, 0],
                     device_id=(t, to), device_id_type=MESH).wait_send()
                 pltpu.make_async_remote_copy(
                     src_ref=psend.at[side], dst_ref=precv.at[side],
@@ -529,11 +536,11 @@
                 pltpu.VMEM((2, FL, W, C), BF),
                 pltpu.VMEM((2, FL, W, C), BF),
                 dma((8,)),
-                dma((RL,)),
+                dma((2,)),
                 dma,
                 dma((6,)),
                 dma((2,)),
-                dma((2, FL, 2)),
+                dma((2, FL)),
                 dma((2,)),
                 dma((2, FL)),
                 pltpu.SemaphoreType.REGULAR,

time: 35.3 us -> 35.2 us (level)
  no operation moved by 1% of the time
where the time goes in v5:
time: 35.2 us; the launch traced here: 34.9 us
  Pallas kernels  34.8 us (99%)
    pallas_call x1, Pallas kernels, local(): pl.pallas_call(lambda *refs: kernel(spaces, *refs), out_shape=pltpu.VMEM(...  33.5 us
    pallas_call x1, Pallas kernels, local(): pl.pallas_call(emit, out_shape=jax.ShapeDtypeStruct(shape, BF), in_specs=...  1.31 us

profile of v5, /device:TPU:96, one launch (start us, length us, event | category | flops | bytes accessed | tf_op | source)
XLA Modules:
  0.0 34.9 jit_solution(7288588228911889184)
XLA Ops:
  0.0 33.5 %fused.1.x = bf16[4,4,256,256]{3,2,1,0:T(8,128)(2,1)S(1)} custom-call(bf16[4,4,256,256]{3,2,1,0:T(8,128)(2,1)} %refs_0_.1, bf16[4,2,128,256]{3,2,1,0:T(8,128)(2,1)} %refs_1_.1, bf16[256,256]{1,0:T(8,128)(2,1)} %refs_2_.1, bf16[256,256]{1,0:T(8,128)(2,1)} %refs_3_.1, bf16[256,256]{1,0:T(8,128)(2,1)} %refs_4_.1, bf16[256,256]{1,0:T(8,128)(2,1)} %refs_5_.1, ...), custom_call_target="tpu_custom_call" | custom-call | tf_op jit(solution)/shard_map/fused/pallas_call | solution.py:511
  33.5 1.3 %emit.1 = bf16[4,4,256,256]{3,2,1,0:T(8,128)(2,1)} custom-call(bf16[4,4,256,256]{3,2,1,0:T(8,128)(2,1)S(1)} %fused.1.x), custom_call_target="tpu_custom_call" | custom-call | tf_op jit(solution)/shard_map/emit/pallas_call | solution.py:559

commit v6 on v5

--- a/solution.py
+++ b/solution.py
@@ -319,8 +319,10 @@
         copy.start()
     edge_units = [(f, r) for f in range(FL) for r in (0, 3)]
     with jax.named_scope("norm03"):
-        normalize(edge_units, 0, 128)
+        normalize(edge_units[1::2], 0, 128)
     norm_copy(1).start()
+    with jax.named_scope("norm0"):
+        normalize(edge_units[0::2], 0, 128)
     norm_copy(0).start()
     with jax.named_scope("weights"):
         loads[1].wait()

time: 35.2 us -> 35 us (level)
  no operation moved by 1% of the time
where the time goes in v6:
time: 35 us; the launch traced here: 34.8 us
  Pallas kernels  34.7 us (99%)
    pallas_call x1, Pallas kernels, local(): pl.pallas_call(lambda *refs: kernel(spaces, *refs), out_shape=pltpu.VMEM(...  33.4 us
    pallas_call x1, Pallas kernels, local(): pl.pallas_call(emit, out_shape=jax.ShapeDtypeStruct(shape, BF), in_specs=...  1.31 us

profile of v6, /device:TPU:96, one launch (start us, length us, event | category | flops | bytes accessed | tf_op | source)
XLA Modules:
  0.0 34.8 jit_solution(575279023609002279)
XLA Ops:
  0.0 33.4 %fused.1.x = bf16[4,4,256,256]{3,2,1,0:T(8,128)(2,1)S(1)} custom-call(bf16[4,4,256,256]{3,2,1,0:T(8,128)(2,1)} %refs_0_.1, bf16[4,2,128,256]{3,2,1,0:T(8,128)(2,1)} %refs_1_.1, bf16[256,256]{1,0:T(8,128)(2,1)} %refs_2_.1, bf16[256,256]{1,0:T(8,128)(2,1)} %refs_3_.1, bf16[256,256]{1,0:T(8,128)(2,1)} %refs_4_.1, bf16[256,256]{1,0:T(8,128)(2,1)} %refs_5_.1, ...), custom_call_target="tpu_custom_call" | custom-call | tf_op jit(solution)/shard_map/fused/pallas_call | solution.py:513
  33.4 1.3 %emit.1 = bf16[4,4,256,256]{3,2,1,0:T(8,128)(2,1)} custom-call(bf16[4,4,256,256]{3,2,1,0:T(8,128)(2,1)S(1)} %fused.1.x), custom_call_target="tpu_custom_call" | custom-call | tf_op jit(solution)/shard_map/emit/pallas_call | solution.py:561
